TPU v7x, 32 devices: a whole 2x2x4 slice. The times are simulated.
32 devices in a mesh: seq: 8 (over z, y), ch: 4 (over x, core).
Axes of the slice: x: 2, y: 2, z: 4, core: 2. Of those that a mesh axis runs over, the one named last changes fastest.
Arguments:
- signal: float32 [1, 65536, 1024], P(None, 'seq', 'ch'), may hold values from -6 to 6
- spectrum: float32 [2, 256, 256, 1024], P(None, 'seq', None, 'ch'), may hold values from -6 to 6
- channel_mode: int32 [1024], P('ch'), may hold values 0 or 1
- skip_gain: float32 [1024], P('ch'), may hold values from -4 to 4
- out_weight: bfloat16 [1024, 1024], P('ch'), may hold values from -0.1875 to 0.1875
Outputs:
- projected: float32 [1, 65536, 1024], P(None, 'seq', 'ch')
Inputs may be any that keep to these rules, and one draw needn't show every extreme that they name: `channel_mode`: 1 marks a channel whose 65536 positions are one sequence, 0 a channel whose positions form a 256 x 256 image.
All inputs are finite; a program needn't handle non-finite values. No bound on the sum of `channel_mode` on one device may be relied on, other than what follows from the above.
Results may differ from a plain program's by a relative error of at most 0.017.
Values may be sent and summed in bfloat16 or wider, within the bound.
A program may use at most 192 MiB of HBM per device.

v0:
```python
import functools

import jax
import jax.numpy as jnp
import numpy as np
from jax import lax
from jax.experimental import pallas as pl
from jax.experimental.pallas import tpu as pltpu
from jax.sharding import PartitionSpec as P

MESH = pl.DeviceIdType.MESH
LANES = 128
AHEAD = 4
BEHIND = 6
LOW = jnp.bfloat16


def phases(row_count, col_count, period):
    product = np.arange(row_count)[:, None] * np.arange(col_count)[None, :] % period
    angles = product * (2.0 * np.pi / period)
    return np.cos(angles), np.sin(angles)


def tables(rows, columns):
    length = rows * columns
    rc, rs = phases(rows, rows, rows)
    cc, cs = phases(columns, columns, columns)
    first = np.concatenate([rc, -rs], 0)
    forward = np.block([[cc, -cs], [cs, cc]])
    backward = np.block([[cc, cs], [-cs, cc]])
    last = np.concatenate([rc, -rs], 1) / length
    twist = phases(rows, columns, length)
    return tuple(jnp.asarray(t, LOW) for t in (first, forward, backward, last)) + tuple(
        jnp.asarray(t, jnp.float32) for t in twist
    )


def dot(a, b):
    return jnp.dot(a, b, preferred_element_type=jnp.float32)


def filter_image(image, real, imag, linear, tables_refs):
    first_ref, forward_ref, backward_ref, last_ref, tc_ref, ts_ref = tables_refs
    rows, columns = tc_ref.shape
    tc = jnp.where(linear, tc_ref[...], 1.0)
    ts = jnp.where(linear, ts_ref[...], 0.0)
    y = dot(first_ref[...], image)
    yr, yi = y[:rows], y[rows:]
    y = jnp.concatenate([(yr * tc + yi * ts).astype(LOW), (yi * tc - yr * ts).astype(LOW)], 1)
    z = dot(y, forward_ref[...])
    zr, zi = z[:, :columns], z[:, columns:]
    fr = real.astype(jnp.float32)
    fi = imag.astype(jnp.float32)
    g = jnp.concatenate([(zr * fr - zi * fi).astype(LOW), (zr * fi + zi * fr).astype(LOW)], 1)
    u = dot(g, backward_ref[...])
    ur, ui = u[:, :columns], u[:, columns:]
    v = jnp.concatenate([(ur * tc - ui * ts).astype(LOW), (ur * ts + ui * tc).astype(LOW)], 0)
    return dot(last_ref[...], v).astype(LOW)


def exchange_kernel(
    n, m, group,
    sig_ref, spec_ref, mode_ref, gain_ref, weight_ref, *rest,
):
    table_hbm = rest[:6]
    hidden_ref, spread_ref = rest[6:8]
    (
        stage, turned, packed, recv, conv, back, lined, hid,
        t0, t1, t2, t3, t4, t5,
        stage_sem, table_sem, send_sem, recv_sem, bsend_sem, brecv_sem,
        gsend_sem, grecv_sem, own_sem, wsend_sem, wrecv_sem, wown_sem,
    ) = rest[8:]
    table_refs = (t0, t1, t2, t3, t4, t5)
    rows_local, columns, owned = sig_ref.shape
    chunk = n * group
    chunks = owned // chunk
    blocks = owned // LANES
    per_block = LANES // chunk
    halves = columns // LANES
    pitch = turned.shape[0] // (halves * rows_local)
    line_pitch = lined.shape[0] // (halves * chunk)
    cols = spread_ref.shape[3]
    me = lax.axis_index("seq")
    mine = lax.axis_index("ch")

    def load(step):
        b, p = divmod(step, 3)
        lanes = pl.ds(b * LANES, LANES)
        src = sig_ref.at[:, :, lanes] if p == 0 else spec_ref.at[p - 1, :, :, lanes]
        return pltpu.make_async_copy(src, stage.at[step % 2], stage_sem.at[step % 2])

    load(0).start()
    load(1).start()
    for k, ref in enumerate(table_refs):
        pltpu.make_async_copy(table_hbm[k], ref, table_sem.at[k]).start()

    barrier = pltpu.get_barrier_semaphore()
    for k in range(1, n):
        pl.semaphore_signal(barrier, 1, device_id=(lax.rem(me + k, n), mine), device_id_type=MESH)
    for k in range(1, m):
        pl.semaphore_signal(barrier, 1, device_id=(me, lax.rem(mine + k, m)), device_id_type=MESH)
    pl.semaphore_wait(barrier, n + m - 2)

    def weight_cols(g):
        return weight_ref.at[:, :, pl.ds(pl.multiple_of(g * cols, LANES), cols)]

    own_weight = pltpu.make_async_copy(weight_cols(mine), spread_ref.at[:, mine], wown_sem)

    def send_weights():
        own_weight.start()
        for k in range(1, m):
            g = lax.rem(mine + k, m)
            pltpu.make_async_remote_copy(
                weight_cols(g), spread_ref.at[:, mine], wsend_sem, wrecv_sem,
                device_id=(me, g), device_id_type=MESH,
            ).start()

    def pack(step):
        b, p = divmod(step, 3)
        load(step).wait()
        slot = step % 2

        def turn(a, carry):
            t = stage[slot, a].T
            for h in range(halves):
                at = pl.multiple_of((h * rows_local + a) * pitch, 8)
                turned[pl.ds(at, LANES), :] = t[:, h * LANES : (h + 1) * LANES]
            return carry

        lax.fori_loop(0, rows_local, turn, 0)

        def split(jj, carry):
            j = b * per_block + jj
            for q in range(chunk):
                for h in range(halves):
                    v = turned[pl.ds(h * rows_local * pitch + jj * chunk + q, rows_local, stride=pitch), :]
                    packed[p, j, q // group, q % group, :, h * LANES : (h + 1) * LANES] = v.astype(LOW)
            recv[p, j, me] = packed[p, j, me]
            return carry

        lax.fori_loop(0, per_block, split, 0)
        if step + 2 < 3 * blocks:
            load(step + 2).start()

    def send(j, planes):
        for k in range(1, n):
            d = lax.rem(me + k, n)
            pltpu.make_async_remote_copy(
                packed.at[planes, j, d], recv.at[planes, j, me], send_sem, recv_sem.at[j],
                device_id=(d, mine), device_id_type=MESH,
            ).start()

    def convolve(j):
        for i in range(group):
            linear = mode_ref[j * chunk + me * group + i] == 1
            planes = [recv[p, j, :, i].reshape(n * rows_local, columns) for p in range(3)]
            out = filter_image(*planes, linear, table_refs)
            conv[j, :, i] = out.reshape(n, rows_local, columns)
        back[j, me] = conv[j, me]
        for k in range(1, n):
            d = lax.rem(me + k, n)
            pltpu.make_async_remote_copy(
                conv.at[j, d], back.at[j, me], bsend_sem, brecv_sem.at[j],
                device_id=(d, mine), device_id_type=MESH,
            ).start()

    def finish(j):
        for q in range(chunk):
            v = back[j, q // group, q % group].astype(jnp.float32)
            x = packed[0, j, q // group, q % group].astype(jnp.float32)
            v = v + gain_ref[j * chunk + q] * x
            for h in range(halves):
                lined[pl.ds((h * chunk + q) * line_pitch, rows_local), :] = v[:, h * LANES : (h + 1) * LANES]
        for a in range(rows_local):
            for h in range(halves):
                v = lined[pl.ds(h * chunk * line_pitch + a, chunk, stride=line_pitch), :]
                hid[j, :, pl.ds(a * columns + h * LANES, LANES)] = v.astype(LOW)
        pltpu.make_async_copy(hid.at[j], hidden_ref.at[j, mine], own_sem).start()
        for k in range(1, m):
            g = lax.rem(mine + k, m)
            pltpu.make_async_remote_copy(
                hid.at[j], hidden_ref.at[j, mine], gsend_sem, grecv_sem,
                device_id=(me, g), device_id_type=MESH,
            ).start()

    def await_bytes(ref, sem):
        pltpu.make_async_copy(ref, ref, sem).wait()

    pack(0)
    for j in range(per_block):
        send(j, pl.ds(0, 1))
    send_weights()
    pack(1)
    pack(2)
    for j in range(AHEAD):
        send(j, pl.ds(1, 2))
    for step in range(3, 3 * blocks):
        pack(step)
    for k, ref in enumerate(table_refs):
        pltpu.make_async_copy(table_hbm[k], ref, table_sem.at[k]).wait()

    def take(j):
        await_bytes(recv.at[:, j, pl.ds(0, n - 1)], recv_sem.at[j])
        convolve(j)

    def put(j):
        await_bytes(back.at[j, pl.ds(0, n - 1)], brecv_sem.at[j])
        finish(j)

    def step(j, carry):
        take(j)

        @pl.when(j + AHEAD < per_block)
        def _():
            send(j + AHEAD, pl.ds(1, 2))

        @pl.when((j + AHEAD >= per_block) & (j + AHEAD < chunks))
        def _():
            send(j + AHEAD, pl.ds(0, 3))

        @pl.when(j >= BEHIND)
        def _():
            put(j - BEHIND)

        return carry

    lax.fori_loop(0, chunks, step, 0)

    def drain(j, carry):
        put(j)
        return carry

    lax.fori_loop(chunks - BEHIND, chunks, drain, 0)
    own_weight.wait()
    await_bytes(hidden_ref.at[:, 0], own_sem)
    await_bytes(packed.at[:, :, pl.ds(0, n - 1)], send_sem)
    await_bytes(conv.at[:, pl.ds(0, n - 1)], bsend_sem)
    await_bytes(spread_ref.at[:, pl.ds(0, m - 1)], wsend_sem)
    await_bytes(spread_ref.at[:, pl.ds(0, m - 1)], wrecv_sem)
    await_bytes(hidden_ref.at[:, pl.ds(0, m - 1)], gsend_sem)
    await_bytes(hidden_ref.at[:, pl.ds(0, m - 1)], grecv_sem)


def exchange(n, m, signal, spectrum, modes, gains, weights, consts):
    rows_local, columns, owned = signal.shape
    rows = rows_local * n
    group = max(1, 16 // n)
    chunk = n * group
    chunks = owned // chunk
    halves = columns // LANES
    cols = weights.shape[2] // m
    pitch = LANES + 8
    line_pitch = rows_local + 8
    hbm = pl.BlockSpec(memory_space=pl.ANY)
    smem = pl.BlockSpec(memory_space=pltpu.SMEM)
    dma = pltpu.SemaphoreType.DMA
    images = (n, group, rows_local, columns)
    return pl.pallas_call(
        functools.partial(exchange_kernel, n, m, group),
        out_shape=(
            jax.ShapeDtypeStruct((chunks, m, chunk, rows_local * columns), LOW),
            jax.ShapeDtypeStruct((chunks, m, chunk, cols), LOW),
        ),
        in_specs=[hbm, hbm, smem, smem, hbm] + [hbm] * 6,
        out_specs=(hbm, hbm),
        scratch_shapes=[
            pltpu.VMEM((2, rows_local, columns, LANES), jnp.float32),
            pltpu.VMEM((halves * rows_local * pitch, LANES), jnp.float32),
            pltpu.VMEM((3, chunks) + images, LOW),
            pltpu.VMEM((3, chunks) + images, LOW),
            pltpu.VMEM((chunks,) + images, LOW),
            pltpu.VMEM((chunks,) + images, LOW),
            pltpu.VMEM((halves * chunk * line_pitch, LANES), jnp.float32),
            pltpu.VMEM((chunks, chunk, rows_local * columns), LOW),
        ]
        + [pltpu.VMEM(t.shape, t.dtype) for t in consts]
        + [
            dma((2,)), dma((6,)), dma(()), dma((chunks,)), dma(()), dma((chunks,)),
            dma(()), dma(()), dma(()), dma(()), dma(()), dma(()),
        ],
        compiler_params=pltpu.CompilerParams(
            collective_id=0, has_side_effects=True, vmem_limit_bytes=62 * 1024 * 1024
        ),
        cost_estimate=pl.CostEstimate(
            flops=owned // n * 24 * rows * rows * columns,
            bytes_accessed=16 * owned * rows_local * columns,
            transcendentals=0,
        ),
        name="exchange",
    )(signal, spectrum, modes, gains, weights, *consts)


def project_kernel(hidden_ref, weight_ref, out_ref):
    depth = weight_ref.shape[0]
    hidden = hidden_ref[...].reshape(depth, out_ref.shape[0])
    out_ref[...] = lax.dot_general(
        hidden, weight_ref[...], (((0,), (0,)), ((), ())), preferred_element_type=jnp.float32
    )


def project(hidden, weights):
    chunks, m, chunk, positions = hidden.shape
    cols = weights.shape[-1]
    tile = 512
    depth = chunks * m * chunk
    return pl.pallas_call(
        project_kernel,
        grid=(positions // tile,),
        in_specs=[
            pl.BlockSpec((chunks, m, chunk, tile), lambda t: (0, 0, 0, t)),
            pl.BlockSpec((depth, cols), lambda t: (0, 0)),
        ],
        out_specs=pl.BlockSpec((tile, cols), lambda t: (t, 0)),
        out_shape=jax.ShapeDtypeStruct((positions, cols), jnp.float32),
        compiler_params=pltpu.CompilerParams(vmem_limit_bytes=32 * 1024 * 1024),
        name="project",
    )(hidden, weights.reshape(depth, cols))


def per_device(signal, spectrum, channel_mode, skip_gain, out_weight):
    n = lax.axis_size("seq")
    m = lax.axis_size("ch")
    batches, local_len, owned = signal.shape
    rows_local, columns = spectrum.shape[1], spectrum.shape[2]
    chunk = n * max(1, 16 // n)
    consts = tables(rows_local * n, columns)
    weights = out_weight.reshape(owned // chunk, chunk, out_weight.shape[1])
    hidden, spread = exchange(
        n, m, signal.reshape(rows_local, columns, owned), spectrum, channel_mode, skip_gain, weights, consts
    )
    out = project(hidden, spread)
    return out.reshape(batches, local_len, out.shape[1])


def solution(mesh):
    placed = (P(None, "seq", "ch"), P(None, "seq", None, "ch"), P("ch"), P("ch"), P("ch", None))
    return jax.shard_map(
        per_device, mesh=mesh, in_specs=placed, out_specs=P(None, "seq", "ch"), check_vma=False
    )
```

profile of v0, /device:TPU:29, one launch (start us, length us, event | category | flops | bytes accessed | tf_op | source)
XLA Modules:
  0.0 456.8 jit_solution(15769288125530513404)
XLA Ops:
  0.0 438.4 %exchange.1 = (bf16[16,4,16,8192]{3,2,1,0:T(8,128)(2,1)}, bf16[16,4,16,256]{3,2,1,0:T(8,128)(2,1)}) custom-call(f32[32,256,256]{2,1,0:T(8,128)} %bitcast.5, f32[2,32,256,256]{3,2,1,0:T(8,128)} %spec_ref.1, s32[256]{0:T(256)} %mode_ref.1, f32[256]{0:T(256)} %gain_ref.1, bf16[16,16,1024]{2,1,0:T(8,128)(2,1)} %bitcast.6, ...), custom_call_target="tpu_custom_call" | custom-call | flops 12884901888 | bytes 33554432 | tf_op jit(solution)/shard_map/exchange/pallas_call | solution.py:258
  438.4 0.0 copy-start
  438.4 5.8 %copy-done = bf16[16,4,16,8192]{3,2,1,0:T(8,128)(2,1)S(1)} copy-done((bf16[16,4,16,8192]{3,2,1,0:T(8,128)(2,1)S(1)}, bf16[16,4,16,8192]{3,2,1,0:T(8,128)(2,1)}, u32[]{:S(2)}) %copy-start) | copy-done | bytes 16777240
  444.2 0.0 copy-start.1
  444.2 1.0 copy-done.1
  445.2 11.5 %project.1 = f32[8192,256]{1,0:T(8,128)} custom-call(bf16[16,4,16,8192]{3,2,1,0:T(8,128)(2,1)S(1)} %copy-done, bf16[1024,256]{1,0:T(8,128)(2,1)S(1)} %bitcast.4), custom_call_target="tpu_custom_call" | custom-call | tf_op jit(solution)/shard_map/project/pallas_call | solution.py:306
Async XLA Ops:
  438.4 5.8 %copy-start = (bf16[16,4,16,8192]{3,2,1,0:T(8,128)(2,1)S(1)}, bf16[16,4,16,8192]{3,2,1,0:T(8,128)(2,1)}, u32[]{:S(2)}) copy-start(bf16[16,4,16,8192]{3,2,1,0:T(8,128)(2,1)} %get-tuple-element.7.hidden_ref) | copy-start | bytes 50331652
  444.2 1.0 copy-start.1
where the time goes:
time: 457 us
  Pallas kernels  450 us (98%)
  local copies, waits for them, and re-layouts  6.8 us (1%)
    pallas_call x1, Pallas kernels, exchange(): pl.pallas_call(functools.partial(exchange_kernel, n, m, group), out_shape...  438 us
    pallas_call x1, Pallas kernels, project(): pl.pallas_call(project_kernel, grid=(positions // tile,), in_specs=[pl.Bl...  11.5 us

commit v1 on v0

--- a/solution.py
+++ b/solution.py
@@ -10,8 +10,8 @@
 
 MESH = pl.DeviceIdType.MESH
 LANES = 128
-AHEAD = 4
-BEHIND = 6
+AHEAD = 2
+BEHIND = 2
 LOW = jnp.bfloat16
 
 
@@ -63,13 +63,13 @@
     sig_ref, spec_ref, mode_ref, gain_ref, weight_ref, *rest,
 ):
     table_hbm = rest[:6]
-    hidden_ref, spread_ref = rest[6:8]
+    total_ref, late_ref, late_weight_ref = rest[6:9]
     (
-        stage, turned, packed, recv, conv, back, lined, hid,
+        stage, turned, packed, recv, back, lined, spread, weights,
         t0, t1, t2, t3, t4, t5,
         stage_sem, table_sem, send_sem, recv_sem, bsend_sem, brecv_sem,
-        gsend_sem, grecv_sem, own_sem, wsend_sem, wrecv_sem, wown_sem,
-    ) = rest[8:]
+        gsend_sem, cross_sem, pair_sem, wsend_sem, wrecv_sem, wown_sem, out_sem,
+    ) = rest[9:]
     table_refs = (t0, t1, t2, t3, t4, t5)
     rows_local, columns, owned = sig_ref.shape
     chunk = n * group
@@ -79,9 +79,14 @@
     halves = columns // LANES
     pitch = turned.shape[0] // (halves * rows_local)
     line_pitch = lined.shape[0] // (halves * chunk)
-    cols = spread_ref.shape[3]
+    cols = weights.shape[3]
+    col_halves = cols // LANES
+    depth = m * chunk
     me = lax.axis_index("seq")
     mine = lax.axis_index("ch")
+    pair = mine + 1 - 2 * lax.rem(mine, 2)
+    across = [lax.rem(mine + 2 * k, m) for k in range(1, m // 2)]
+    conv = recv.at[0]
 
     def load(step):
         b, p = divmod(step, 3)
@@ -91,35 +96,29 @@
 
     load(0).start()
     load(1).start()
-    for k, ref in enumerate(table_refs):
-        pltpu.make_async_copy(table_hbm[k], ref, table_sem.at[k]).start()
-
     barrier = pltpu.get_barrier_semaphore()
     for k in range(1, n):
         pl.semaphore_signal(barrier, 1, device_id=(lax.rem(me + k, n), mine), device_id_type=MESH)
     for k in range(1, m):
         pl.semaphore_signal(barrier, 1, device_id=(me, lax.rem(mine + k, m)), device_id_type=MESH)
-    pl.semaphore_wait(barrier, n + m - 2)
+    for k, ref in enumerate(table_refs):
+        pltpu.make_async_copy(table_hbm[k], ref, table_sem.at[k]).start()
 
     def weight_cols(g):
         return weight_ref.at[:, :, pl.ds(pl.multiple_of(g * cols, LANES), cols)]
 
-    own_weight = pltpu.make_async_copy(weight_cols(mine), spread_ref.at[:, mine], wown_sem)
+    own_weight = pltpu.make_async_copy(weight_cols(mine), weights.at[:, mine], wown_sem)
 
     def send_weights():
         own_weight.start()
         for k in range(1, m):
             g = lax.rem(mine + k, m)
             pltpu.make_async_remote_copy(
-                weight_cols(g), spread_ref.at[:, mine], wsend_sem, wrecv_sem,
+                weight_cols(g), weights.at[:, mine], wsend_sem, wrecv_sem,
                 device_id=(me, g), device_id_type=MESH,
             ).start()
 
-    def pack(step):
-        b, p = divmod(step, 3)
-        load(step).wait()
-        slot = step % 2
-
+    def turn_all(slot):
         def turn(a, carry):
             t = stage[slot, a].T
             for h in range(halves):
@@ -129,6 +128,7 @@
 
         lax.fori_loop(0, rows_local, turn, 0)
 
+    def split_all(b, p, after):
         def split(jj, carry):
             j = b * per_block + jj
             for q in range(chunk):
@@ -136,11 +136,21 @@
                     v = turned[pl.ds(h * rows_local * pitch + jj * chunk + q, rows_local, stride=pitch), :]
                     packed[p, j, q // group, q % group, :, h * LANES : (h + 1) * LANES] = v.astype(LOW)
             recv[p, j, me] = packed[p, j, me]
+            if after is not None:
+                after(j)
             return carry
 
         lax.fori_loop(0, per_block, split, 0)
+
+    def pack(step, before=None, after=None):
+        b, p = divmod(step, 3)
+        load(step).wait()
+        turn_all(step % 2)
+        if before is not None:
+            before()
         if step + 2 < 3 * blocks:
             load(step + 2).start()
+        split_all(b, p, after)
 
     def send(j, planes):
         for k in range(1, n):
@@ -164,6 +174,11 @@
                 device_id=(d, mine), device_id_type=MESH,
             ).start()
 
+    def give(j, g, to, sem):
+        pltpu.make_async_remote_copy(
+            spread.at[j, g], spread.at[j, g], gsend_sem, sem, device_id=(me, to), device_id_type=MESH
+        ).start()
+
     def finish(j):
         for q in range(chunk):
             v = back[j, q // group, q % group].astype(jnp.float32)
@@ -174,21 +189,46 @@
         for a in range(rows_local):
             for h in range(halves):
                 v = lined[pl.ds(h * chunk * line_pitch + a, chunk, stride=line_pitch), :]
-                hid[j, :, pl.ds(a * columns + h * LANES, LANES)] = v.astype(LOW)
-        pltpu.make_async_copy(hid.at[j], hidden_ref.at[j, mine], own_sem).start()
-        for k in range(1, m):
-            g = lax.rem(mine + k, m)
-            pltpu.make_async_remote_copy(
-                hid.at[j], hidden_ref.at[j, mine], gsend_sem, grecv_sem,
-                device_id=(me, g), device_id_type=MESH,
-            ).start()
+                spread[j, mine, :, pl.ds(a * columns + h * LANES, LANES)] = v.astype(LOW)
+        for g in across:
+            give(j, mine, g, cross_sem.at[j])
+        give(j, mine, pair, pair_sem.at[j])
 
     def await_bytes(ref, sem):
         pltpu.make_async_copy(ref, ref, sem).wait()
 
-    pack(0)
-    for j in range(per_block):
-        send(j, pl.ds(0, 1))
+    def take(j):
+        await_bytes(recv.at[:, j, pl.ds(0, n - 1)], recv_sem.at[j])
+        convolve(j)
+
+    def put(j):
+        await_bytes(back.at[j, pl.ds(0, n - 1)], brecv_sem.at[j])
+        finish(j)
+
+    def forward(j):
+        if across:
+            await_bytes(spread.at[j, pl.ds(0, len(across))], cross_sem.at[j])
+        for g in across:
+            give(j, g, pair, pair_sem.at[j])
+
+    def gathered(j):
+        await_bytes(spread.at[j, pl.ds(0, m // 2)], pair_sem.at[j])
+
+    def accumulate(j):
+        gathered(j)
+        w = weights[j].reshape(depth, cols)
+
+        def tile(a, carry):
+            at = pl.multiple_of(a * columns, LANES)
+            v = spread[j, :, :, pl.ds(at, columns)].reshape(depth, columns)
+            v = lax.dot_general(v, w, (((0,), (0,)), ((), ())), preferred_element_type=jnp.float32)
+            for h in range(col_halves):
+                stage[h, a] += v[:, h * LANES : (h + 1) * LANES]
+            return carry
+
+        lax.fori_loop(0, rows_local, tile, 0)
+
+    pack(0, before=lambda: pl.semaphore_wait(barrier, n + m - 2), after=lambda j: send(j, pl.ds(0, 1)))
     send_weights()
     pack(1)
     pack(2)
@@ -198,14 +238,10 @@
         pack(step)
     for k, ref in enumerate(table_refs):
         pltpu.make_async_copy(table_hbm[k], ref, table_sem.at[k]).wait()
-
-    def take(j):
-        await_bytes(recv.at[:, j, pl.ds(0, n - 1)], recv_sem.at[j])
-        convolve(j)
-
-    def put(j):
-        await_bytes(back.at[j, pl.ds(0, n - 1)], brecv_sem.at[j])
-        finish(j)
+    own_weight.wait()
+    await_bytes(weights.at[:, pl.ds(0, m - 1)], wrecv_sem)
+    for h in range(col_halves):
+        stage[h] = jnp.zeros(stage.shape[1:], stage.dtype)
 
     def step(j, carry):
         take(j)
@@ -222,23 +258,51 @@
         def _():
             put(j - BEHIND)
 
+        @pl.when(j >= BEHIND + 1)
+        def _():
+            forward(j - BEHIND - 1)
+
+        @pl.when(j >= BEHIND + 2)
+        def _():
+            accumulate(j - BEHIND - 2)
+
         return carry
 
     lax.fori_loop(0, chunks, step, 0)
 
     def drain(j, carry):
         put(j)
+
+        @pl.when(j >= 1)
+        def _():
+            forward(j - 1)
+
+        @pl.when(j >= 2)
+        def _():
+            accumulate(j - 2)
+
         return carry
 
     lax.fori_loop(chunks - BEHIND, chunks, drain, 0)
-    own_weight.wait()
-    await_bytes(hidden_ref.at[:, 0], own_sem)
+    last = chunks - 1
+    accumulate(last - 1)
+    outs = [
+        pltpu.make_async_copy(stage.at[h], total_ref.at[:, :, pl.ds(h * LANES, LANES)], out_sem)
+        for h in range(col_halves)
+    ]
+    outs.append(pltpu.make_async_copy(weights.at[last], late_weight_ref, out_sem))
+    for copy in outs:
+        copy.start()
+    forward(last)
+    gathered(last)
+    outs.append(pltpu.make_async_copy(spread.at[last], late_ref, out_sem))
+    outs[-1].start()
     await_bytes(packed.at[:, :, pl.ds(0, n - 1)], send_sem)
     await_bytes(conv.at[:, pl.ds(0, n - 1)], bsend_sem)
-    await_bytes(spread_ref.at[:, pl.ds(0, m - 1)], wsend_sem)
-    await_bytes(spread_ref.at[:, pl.ds(0, m - 1)], wrecv_sem)
-    await_bytes(hidden_ref.at[:, pl.ds(0, m - 1)], gsend_sem)
-    await_bytes(hidden_ref.at[:, pl.ds(0, m - 1)], grecv_sem)
+    await_bytes(weights.at[:, pl.ds(0, m - 1)], wsend_sem)
+    await_bytes(spread.at[:, pl.ds(0, m - 1)], gsend_sem)
+    for copy in outs:
+        copy.wait()
 
 
 def exchange(n, m, signal, spectrum, modes, gains, weights, consts):
@@ -258,28 +322,29 @@
     return pl.pallas_call(
         functools.partial(exchange_kernel, n, m, group),
         out_shape=(
-            jax.ShapeDtypeStruct((chunks, m, chunk, rows_local * columns), LOW),
-            jax.ShapeDtypeStruct((chunks, m, chunk, cols), LOW),
+            jax.ShapeDtypeStruct((rows_local, columns, cols), jnp.float32),
+            jax.ShapeDtypeStruct((m, chunk, rows_local * columns), LOW),
+            jax.ShapeDtypeStruct((m, chunk, cols), LOW),
         ),
         in_specs=[hbm, hbm, smem, smem, hbm] + [hbm] * 6,
-        out_specs=(hbm, hbm),
+        out_specs=(hbm, hbm, hbm),
         scratch_shapes=[
             pltpu.VMEM((2, rows_local, columns, LANES), jnp.float32),
             pltpu.VMEM((halves * rows_local * pitch, LANES), jnp.float32),
             pltpu.VMEM((3, chunks) + images, LOW),
             pltpu.VMEM((3, chunks) + images, LOW),
             pltpu.VMEM((chunks,) + images, LOW),
-            pltpu.VMEM((chunks,) + images, LOW),
             pltpu.VMEM((halves * chunk * line_pitch, LANES), jnp.float32),
-            pltpu.VMEM((chunks, chunk, rows_local * columns), LOW),
+            pltpu.VMEM((chunks, m, chunk, rows_local * columns), LOW),
+            pltpu.VMEM((chunks, m, chunk, cols), LOW),
         ]
         + [pltpu.VMEM(t.shape, t.dtype) for t in consts]
         + [
             dma((2,)), dma((6,)), dma(()), dma((chunks,)), dma(()), dma((chunks,)),
-            dma(()), dma(()), dma(()), dma(()), dma(()), dma(()),
+            dma(()), dma((chunks,)), dma((chunks,)), dma(()), dma(()), dma(()), dma(()),
         ],
         compiler_params=pltpu.CompilerParams(
-            collective_id=0, has_side_effects=True, vmem_limit_bytes=62 * 1024 * 1024
+            collective_id=0, has_side_effects=True, vmem_limit_bytes=63 * 1024 * 1024
         ),
         cost_estimate=pl.CostEstimate(
             flops=owned // n * 24 * rows * rows * columns,
@@ -290,31 +355,32 @@
     )(signal, spectrum, modes, gains, weights, *consts)
 
 
-def project_kernel(hidden_ref, weight_ref, out_ref):
+def project_kernel(total_ref, hidden_ref, weight_ref, out_ref):
     depth = weight_ref.shape[0]
     hidden = hidden_ref[...].reshape(depth, out_ref.shape[0])
-    out_ref[...] = lax.dot_general(
+    out_ref[...] = total_ref[...] + lax.dot_general(
         hidden, weight_ref[...], (((0,), (0,)), ((), ())), preferred_element_type=jnp.float32
     )
 
 
-def project(hidden, weights):
-    chunks, m, chunk, positions = hidden.shape
+def project(total, hidden, weights):
+    m, chunk, positions = hidden.shape
     cols = weights.shape[-1]
-    tile = 512
-    depth = chunks * m * chunk
+    tile = 1024
+    depth = m * chunk
     return pl.pallas_call(
         project_kernel,
         grid=(positions // tile,),
         in_specs=[
-            pl.BlockSpec((chunks, m, chunk, tile), lambda t: (0, 0, 0, t)),
+            pl.BlockSpec((tile, cols), lambda t: (t, 0)),
+            pl.BlockSpec((m, chunk, tile), lambda t: (0, 0, t)),
             pl.BlockSpec((depth, cols), lambda t: (0, 0)),
         ],
         out_specs=pl.BlockSpec((tile, cols), lambda t: (t, 0)),
         out_shape=jax.ShapeDtypeStruct((positions, cols), jnp.float32),
-        compiler_params=pltpu.CompilerParams(vmem_limit_bytes=32 * 1024 * 1024),
+        compiler_params=pltpu.CompilerParams(vmem_limit_bytes=63 * 1024 * 1024),
         name="project",
-    )(hidden, weights.reshape(depth, cols))
+    )(total.reshape(positions, cols), hidden, weights.reshape(depth, cols))
 
 
 def per_device(signal, spectrum, channel_mode, skip_gain, out_weight):
@@ -325,10 +391,10 @@
     chunk = n * max(1, 16 // n)
     consts = tables(rows_local * n, columns)
     weights = out_weight.reshape(owned // chunk, chunk, out_weight.shape[1])
-    hidden, spread = exchange(
+    late = exchange(
         n, m, signal.reshape(rows_local, columns, owned), spectrum, channel_mode, skip_gain, weights, consts
     )
-    out = project(hidden, spread)
+    out = project(*late)
     return out.reshape(batches, local_len, out.shape[1])
 
 

time: 457 us -> 408 us (0.89)
  Pallas kernels: 450 us -> 405 us
  local copies, waits for them, and re-layouts: 6.8 us -> 0 us
    pallas_call x1, Pallas kernels: 438 us -> 395 us  [exchange(): pl.pallas_call(functools.partial(exchange_kernel, n, m, group), out_shape...]
    unnamed x4 -> x0, local copies, waits for them, and re-layouts: 6.8 us -> none
where the time goes in v1:
time: 408 us; the launch traced here: 405 us
  Pallas kernels  405 us (99%)
    pallas_call x1, Pallas kernels, exchange(): pl.pallas_call(functools.partial(exchange_kernel, n, m, group), out_shape...  395 us
    pallas_call x1, Pallas kernels, project(): pl.pallas_call(project_kernel, grid=(positions // tile,), in_specs=[pl.Bl...  9.94 us

profile of v1, /device:TPU:29, one launch (start us, length us, event | category | flops | bytes accessed | tf_op | source)
XLA Modules:
  0.0 405.4 jit_solution(7914462763717057075)
XLA Ops:
  0.0 395.5 %exchange.1 = (f32[32,256,256]{2,1,0:T(8,128)}, bf16[4,16,8192]{2,1,0:T(8,128)(2,1)}, bf16[4,16,256]{2,1,0:T(8,128)(2,1)}) custom-call(f32[32,256,256]{2,1,0:T(8,128)} %bitcast.7, f32[2,32,256,256]{3,2,1,0:T(8,128)} %spec_ref.1, s32[256]{0:T(256)} %mode_ref.1, f32[256]{0:T(256)} %gain_ref.1, bf16[16,16,1024]{2,1,0:T(8,128)(2,1)} %bitcast.8, ...), custom_call_target="tpu_custom_call" | custom-call | flops 12884901888 | bytes 33554432 | tf_op jit(solution)/shard_map/exchange/pallas_call | solution.py:322
  395.5 9.9 %project.1 = f32[8192,256]{1,0:T(8,128)} custom-call(f32[8192,256]{1,0:T(8,128)} %bitcast.5, bf16[4,16,8192]{2,1,0:T(8,128)(2,1)} %get-tuple-element.9.hidden_ref, bf16[64,256]{1,0:T(8,128)(2,1)} %bitcast.6), custom_call_target="tpu_custom_call" | custom-call | tf_op jit(solution)/shard_map/project/pallas_call | solution.py:371

commit v2 on v1

--- a/solution.py
+++ b/solution.py
@@ -12,6 +12,8 @@
 LANES = 128
 AHEAD = 2
 BEHIND = 2
+SPAN = 16
+VMEM_BYTES = 55 * 1024 * 1024
 LOW = jnp.bfloat16
 
 
@@ -63,13 +65,13 @@
     sig_ref, spec_ref, mode_ref, gain_ref, weight_ref, *rest,
 ):
     table_hbm = rest[:6]
-    total_ref, late_ref, late_weight_ref = rest[6:9]
+    total_ref = rest[6]
     (
-        stage, turned, packed, recv, back, lined, spread, weights,
+        turned, packed, recv, back, lined, spread, weights,
         t0, t1, t2, t3, t4, t5,
         stage_sem, table_sem, send_sem, recv_sem, bsend_sem, brecv_sem,
-        gsend_sem, cross_sem, pair_sem, wsend_sem, wrecv_sem, wown_sem, out_sem,
-    ) = rest[9:]
+        gsend_sem, cross_sem, pair_sem, wsend_sem, wrecv_sem, wown_sem,
+    ) = rest[7:]
     table_refs = (t0, t1, t2, t3, t4, t5)
     rows_local, columns, owned = sig_ref.shape
     chunk = n * group
@@ -80,19 +82,20 @@
     pitch = turned.shape[0] // (halves * rows_local)
     line_pitch = lined.shape[0] // (halves * chunk)
     cols = weights.shape[3]
-    col_halves = cols // LANES
     depth = m * chunk
+    span = min(SPAN, rows_local)
     me = lax.axis_index("seq")
     mine = lax.axis_index("ch")
     pair = mine + 1 - 2 * lax.rem(mine, 2)
     across = [lax.rem(mine + 2 * k, m) for k in range(1, m // 2)]
     conv = recv.at[0]
+    stage = [total_ref.at[:, :, pl.ds(h * LANES, LANES)] for h in range(2)]
 
     def load(step):
         b, p = divmod(step, 3)
         lanes = pl.ds(b * LANES, LANES)
         src = sig_ref.at[:, :, lanes] if p == 0 else spec_ref.at[p - 1, :, :, lanes]
-        return pltpu.make_async_copy(src, stage.at[step % 2], stage_sem.at[step % 2])
+        return pltpu.make_async_copy(src, stage[step % 2], stage_sem.at[step % 2])
 
     load(0).start()
     load(1).start()
@@ -120,7 +123,7 @@
 
     def turn_all(slot):
         def turn(a, carry):
-            t = stage[slot, a].T
+            t = stage[slot][a].T
             for h in range(halves):
                 at = pl.multiple_of((h * rows_local + a) * pitch, 8)
                 turned[pl.ds(at, LANES), :] = t[:, h * LANES : (h + 1) * LANES]
@@ -219,14 +222,13 @@
         w = weights[j].reshape(depth, cols)
 
         def tile(a, carry):
-            at = pl.multiple_of(a * columns, LANES)
-            v = spread[j, :, :, pl.ds(at, columns)].reshape(depth, columns)
+            at = pl.multiple_of(a * span * columns, LANES)
+            v = spread[j, :, :, pl.ds(at, span * columns)].reshape(depth, span * columns)
             v = lax.dot_general(v, w, (((0,), (0,)), ((), ())), preferred_element_type=jnp.float32)
-            for h in range(col_halves):
-                stage[h, a] += v[:, h * LANES : (h + 1) * LANES]
+            total_ref[pl.ds(a * span, span), :, :cols] += v.reshape(span, columns, cols)
             return carry
 
-        lax.fori_loop(0, rows_local, tile, 0)
+        lax.fori_loop(0, rows_local // span, tile, 0)
 
     pack(0, before=lambda: pl.semaphore_wait(barrier, n + m - 2), after=lambda j: send(j, pl.ds(0, 1)))
     send_weights()
@@ -240,8 +242,7 @@
         pltpu.make_async_copy(table_hbm[k], ref, table_sem.at[k]).wait()
     own_weight.wait()
     await_bytes(weights.at[:, pl.ds(0, m - 1)], wrecv_sem)
-    for h in range(col_halves):
-        stage[h] = jnp.zeros(stage.shape[1:], stage.dtype)
+    total_ref[...] = jnp.zeros(total_ref.shape, total_ref.dtype)
 
     def step(j, carry):
         take(j)
@@ -286,23 +287,12 @@
     lax.fori_loop(chunks - BEHIND, chunks, drain, 0)
     last = chunks - 1
     accumulate(last - 1)
-    outs = [
-        pltpu.make_async_copy(stage.at[h], total_ref.at[:, :, pl.ds(h * LANES, LANES)], out_sem)
-        for h in range(col_halves)
-    ]
-    outs.append(pltpu.make_async_copy(weights.at[last], late_weight_ref, out_sem))
-    for copy in outs:
-        copy.start()
     forward(last)
-    gathered(last)
-    outs.append(pltpu.make_async_copy(spread.at[last], late_ref, out_sem))
-    outs[-1].start()
+    accumulate(last)
     await_bytes(packed.at[:, :, pl.ds(0, n - 1)], send_sem)
     await_bytes(conv.at[:, pl.ds(0, n - 1)], bsend_sem)
     await_bytes(weights.at[:, pl.ds(0, m - 1)], wsend_sem)
     await_bytes(spread.at[:, pl.ds(0, m - 1)], gsend_sem)
-    for copy in outs:
-        copy.wait()
 
 
 def exchange(n, m, signal, spectrum, modes, gains, weights, consts):
@@ -321,15 +311,10 @@
     images = (n, group, rows_local, columns)
     return pl.pallas_call(
         functools.partial(exchange_kernel, n, m, group),
-        out_shape=(
-            jax.ShapeDtypeStruct((rows_local, columns, cols), jnp.float32),
-            jax.ShapeDtypeStruct((m, chunk, rows_local * columns), LOW),
-            jax.ShapeDtypeStruct((m, chunk, cols), LOW),
-        ),
+        out_shape=pltpu.VMEM((rows_local, columns, max(cols, 2 * LANES)), jnp.float32),
         in_specs=[hbm, hbm, smem, smem, hbm] + [hbm] * 6,
-        out_specs=(hbm, hbm, hbm),
+        out_specs=pl.BlockSpec(memory_space=pltpu.VMEM),
         scratch_shapes=[
-            pltpu.VMEM((2, rows_local, columns, LANES), jnp.float32),
             pltpu.VMEM((halves * rows_local * pitch, LANES), jnp.float32),
             pltpu.VMEM((3, chunks) + images, LOW),
             pltpu.VMEM((3, chunks) + images, LOW),
@@ -341,10 +326,10 @@
         + [pltpu.VMEM(t.shape, t.dtype) for t in consts]
         + [
             dma((2,)), dma((6,)), dma(()), dma((chunks,)), dma(()), dma((chunks,)),
-            dma(()), dma((chunks,)), dma((chunks,)), dma(()), dma(()), dma(()), dma(()),
+            dma(()), dma((chunks,)), dma((chunks,)), dma(()), dma(()), dma(()),
         ],
         compiler_params=pltpu.CompilerParams(
-            collective_id=0, has_side_effects=True, vmem_limit_bytes=63 * 1024 * 1024
+            collective_id=0, has_side_effects=True, vmem_limit_bytes=VMEM_BYTES
         ),
         cost_estimate=pl.CostEstimate(
             flops=owned // n * 24 * rows * rows * columns,
@@ -355,34 +340,6 @@
     )(signal, spectrum, modes, gains, weights, *consts)
 
 
-def project_kernel(total_ref, hidden_ref, weight_ref, out_ref):
-    depth = weight_ref.shape[0]
-    hidden = hidden_ref[...].reshape(depth, out_ref.shape[0])
-    out_ref[...] = total_ref[...] + lax.dot_general(
-        hidden, weight_ref[...], (((0,), (0,)), ((), ())), preferred_element_type=jnp.float32
-    )
-
-
-def project(total, hidden, weights):
-    m, chunk, positions = hidden.shape
-    cols = weights.shape[-1]
-    tile = 1024
-    depth = m * chunk
-    return pl.pallas_call(
-        project_kernel,
-        grid=(positions // tile,),
-        in_specs=[
-            pl.BlockSpec((tile, cols), lambda t: (t, 0)),
-            pl.BlockSpec((m, chunk, tile), lambda t: (0, 0, t)),
-            pl.BlockSpec((depth, cols), lambda t: (0, 0)),
-        ],
-        out_specs=pl.BlockSpec((tile, cols), lambda t: (t, 0)),
-        out_shape=jax.ShapeDtypeStruct((positions, cols), jnp.float32),
-        compiler_params=pltpu.CompilerParams(vmem_limit_bytes=63 * 1024 * 1024),
-        name="project",
-    )(total.reshape(positions, cols), hidden, weights.reshape(depth, cols))
-
-
 def per_device(signal, spectrum, channel_mode, skip_gain, out_weight):
     n = lax.axis_size("seq")
     m = lax.axis_size("ch")
@@ -391,11 +348,10 @@
     chunk = n * max(1, 16 // n)
     consts = tables(rows_local * n, columns)
     weights = out_weight.reshape(owned // chunk, chunk, out_weight.shape[1])
-    late = exchange(
+    out = exchange(
         n, m, signal.reshape(rows_local, columns, owned), spectrum, channel_mode, skip_gain, weights, consts
     )
-    out = project(*late)
-    return out.reshape(batches, local_len, out.shape[1])
+    return out[..., : out_weight.shape[1] // m].reshape(batches, local_len, out_weight.shape[1] // m)
 
 
 def solution(mesh):

time: 408 us -> 391 us (0.958)
  Pallas kernels: 405 us -> 385 us
    pallas_call x1, Pallas kernels: 395 us -> 385 us  [exchange(): pl.pallas_call(functools.partial(exchange_kernel, n, m, group), out_shape...]
    pallas_call x1 -> x0, Pallas kernels: 9.94 us -> none  [project(): pl.pallas_call(project_kernel, grid=(positions // tile,), in_specs=[pl.Bl...]
where the time goes in v2:
time: 391 us; the launch traced here: 388 us
  Pallas kernels  385 us (98%)
    pallas_call x1, Pallas kernels, exchange(): pl.pallas_call(functools.partial(exchange_kernel, n, m, group), out_shape...  385 us

profile of v2, /device:TPU:29, one launch (start us, length us, event | category | flops | bytes accessed | tf_op | source)
XLA Modules:
  0.0 388.1 jit_solution(12125372398006263080)
XLA Ops:
  0.0 384.6 %exchange.1 = f32[32,256,256]{2,1,0:T(8,128)S(1)} custom-call(f32[32,256,256]{2,1,0:T(8,128)} %bitcast.4, f32[2,32,256,256]{3,2,1,0:T(8,128)} %spec_ref.1, s32[256]{0:T(256)} %mode_ref.1, f32[256]{0:T(256)} %gain_ref.1, bf16[16,16,1024]{2,1,0:T(8,128)(2,1)} %bitcast.5, bf16[512,256]{1,0:T(8,128)(2,1)} %constant.12.clone.rest_0_, ...), custom_call_target="tpu_custom_call" | custom-call | flops 12884901888 | bytes 33554432 | tf_op jit(solution)/shard_map/exchange/pallas_call | solution.py:312
  384.7 3.4 copy.13
